TPU v7x, 256 devices: a whole 4x4x8 slice. The times are simulated.
256 devices in a mesh: rows: 8 (over z), feat: 32 (over y, x, core).
Axes of the slice: x: 4, y: 4, z: 8, core: 2. Of those that a mesh axis runs over, the one named last changes fastest.
Arguments:
- codes: int32 [524288, 512], P(('rows', 'feat')), may hold values from 0 to 255, as said below
- node_ids: int32 [2, 524288], P(None, ('rows', 'feat')), may hold values from 0 to 3
- bag_counts: int32 [2, 524288], P(None, ('rows', 'feat')), may hold values from 0 to 3
- labels: int32 [524288], P(('rows', 'feat')), may hold values from 0 to 1
Outputs:
- feature_gain: float32 [2, 4, 512], P(None, None, 'feat')
- node_gain: float32 [2, 4], replicated
Inputs may be any that keep to these rules, and one draw needn't show every extreme that they name: Each feature's codes lie below a cap of that feature; bins above the cap are empty.
All inputs are finite; a program needn't handle non-finite values.
Results may differ from a plain program's by a relative error of at most 0.0003.
Values sent between devices are 32-bit elements; how exact they have to be, the bound alone decides.
A program may use at most 64 MiB of HBM per device.

v0:
```python
import math

import jax
import jax.numpy as jnp
from jax import lax
from jax.sharding import PartitionSpec as P

BINS = 256
CLASSES = 2
TREES = 2
NODES = 4


def over_pieces(array, axis):
    return lax.all_gather(array, axis).sum(0)


def from_everyone(array, axis):
    count = lax.axis_size(axis)
    return lax.all_to_all(
        jnp.broadcast_to(array[None], (count, *array.shape)), axis, 0, 0, tiled=True
    )


def of_everyone(array, axis):
    return from_everyone(array, axis).max(axis=0)


def make_weights(node_ids, bag_counts, labels):
    trees, count_rows = node_ids.shape
    node_range = jnp.arange(NODES, dtype=jnp.int32)
    class_range = jnp.arange(CLASSES, dtype=jnp.int32)
    node_hit = (node_ids[:, :, None] == node_range).astype(jnp.float32)
    class_hit = (labels[:, None] == class_range).astype(jnp.float32)
    weights = (
        bag_counts.astype(jnp.float32)[:, :, None, None]
        * node_hit[:, :, :, None]
        * class_hit[None, :, None, :]
    )
    return (
        jnp.transpose(weights, (1, 0, 2, 3))
        .reshape(count_rows, trees * NODES * CLASSES)
        .astype(jnp.bfloat16)
    )


def split_gains(left):
    feats = left.shape[0]
    left = left.reshape(feats, TREES, NODES, CLASSES, left.shape[-1])
    total = left[..., -1:]
    n_left = jnp.sum(left, axis=3, keepdims=True)
    n_total = jnp.sum(total, axis=3, keepdims=True)
    n_right = n_total - n_left
    frac = n_left / jnp.maximum(n_total, 1.0)
    spread_terms = (left - total * frac) ** 2
    scaled = n_total / (jnp.maximum(n_left, 1.0) * jnp.maximum(n_right, 1.0))
    spread = jnp.sum(spread_terms * scaled, axis=3)
    best = jnp.max(spread, axis=-1)
    return jnp.transpose(best, (1, 2, 0))


def gains_of(hist):
    bin_index = jnp.arange(BINS, dtype=jnp.int32)
    upper = (bin_index[:, None] <= bin_index[None, :]).astype(jnp.float32)
    left = jnp.einsum("fsb,bk->fsk", hist, upper, precision=lax.Precision.HIGHEST)
    return split_gains(left)


def histogram_of(columns, weights):
    count_rows, count = columns.shape
    block_size = math.gcd(count, 32)
    blocks = jnp.transpose(columns.reshape(count_rows, count // block_size, block_size), (1, 0, 2))
    bin_index = jnp.arange(BINS, dtype=jnp.int32)

    def one_block(column_block):
        onehot = (column_block[:, :, None] == bin_index).astype(jnp.bfloat16)
        return jnp.einsum("rfb,rs->fsb", onehot, weights, preferred_element_type=jnp.float32)

    summed = lax.map(one_block, blocks)
    return summed.reshape(count, weights.shape[1], BINS)


def on_device(codes, node_ids, bag_counts, labels):
    weights = make_weights(node_ids, bag_counts, labels)
    partial_hist = lax.psum_scatter(
        histogram_of(codes, weights), "feat", scatter_dimension=0, tiled=True
    )
    hist = over_pieces(partial_hist, "rows")
    feature_gain = gains_of(hist)
    node_gain = of_everyone(jnp.max(feature_gain, axis=2), "feat")
    return (feature_gain, node_gain)


def solution(mesh):
    return jax.shard_map(
        on_device,
        mesh=mesh,
        in_specs=(
            P(("rows", "feat"), None),
            P(None, ("rows", "feat")),
            P(None, ("rows", "feat")),
            P(("rows", "feat")),
        ),
        out_specs=(P(None, None, "feat"), P()),
        check_vma=False,
    )
```

profile of v0, /device:TPU:1, one launch (start us, length us, event | category | flops | bytes accessed | tf_op | source)
XLA Modules:
  0.0 470.8 jit_solution(1018175916903868701)
XLA Ops:
  7.2 5.4 %copy.18 = s32[2048,512]{0,1:T(8,128)} copy(s32[2048,512]{1,0:T(8,128)} %param.6) | data formatting | bytes 8388608 | tf_op args[0]
  12.8 286.6 %while.11 = (s32[]{:T(128)}, f32[16,32,16,256]{3,2,1,0:T(8,128)}, s32[16,2048,32]{1,2,0:T(8,128)}, f32[2048,2]{0,1:T(2,128)S(1)}, f32[2048,2,4]{0,2,1:T(4,128)S(1)}, /*index=5*/s32[]{:T(128)}) while((s32[]{:T(128)}, f32[16,32,16,256]{3,2,1,0:T(8,128)}, s32[16,2048,32]{1,2,0:T(8,128)}, f32[2048,2]{0,1:T(2,128)S(1)}, ...), condition=%wide.region_1.2_spmd.clone, body=%wide.region_0.1_spmd.clone.sunk | while | flops 553713664 | bytes 1655369 | solution.py:79
  12.8 1.0 dynamic-slice_bitcast_fusion.2
  13.8 0.1 multiply_convert_fusion.2
  13.9 16.8 %fusion.20 = f32[16,32,16,256]{3,2,1,0:T(8,128)} fusion(f32[16,32,16,256]{3,2,1,0:T(8,128)} %get-tuple-element.99, s32[]{:T(128)} %get-tuple-element.98, bf16[2048,16,1]{0,1,2:T(8,128)(2,1)S(1)} %reshape.85, s32[2048,32]{0,1:T(8,128)S(1)} %dynamic-slice_bitcast_fusion.2), kind=kOutput, calls=%fused_computation.6.clone.2 | convolution fusion | flops 553648128 | bytes 852480 | tf_op jit(solution)/shard_map/while/body/eval_jaxpr/rfb,rs->fsb/dot_general | solution.py:77
  30.7 1.0 dynamic-slice_bitcast_fusion.2
  31.8 16.8 %fusion.20 = f32[16,32,16,256]{3,2,1,0:T(8,128)} fusion(f32[16,32,16,256]{3,2,1,0:T(8,128)} %get-tuple-element.99, s32[]{:T(128)} %get-tuple-element.98, bf16[2048,16,1]{0,1,2:T(8,128)(2,1)S(1)} %reshape.85, s32[2048,32]{0,1:T(8,128)S(1)} %dynamic-slice_bitcast_fusion.2), kind=kOutput, calls=%fused_computation.6.clone.2 | convolution fusion | flops 553648128 | bytes 852480 | tf_op jit(solution)/shard_map/while/body/eval_jaxpr/rfb,rs->fsb/dot_general | solution.py:77
  48.6 1.0 dynamic-slice_bitcast_fusion.2
  49.7 16.8 %fusion.20 = f32[16,32,16,256]{3,2,1,0:T(8,128)} fusion(f32[16,32,16,256]{3,2,1,0:T(8,128)} %get-tuple-element.99, s32[]{:T(128)} %get-tuple-element.98, bf16[2048,16,1]{0,1,2:T(8,128)(2,1)S(1)} %reshape.85, s32[2048,32]{0,1:T(8,128)S(1)} %dynamic-slice_bitcast_fusion.2), kind=kOutput, calls=%fused_computation.6.clone.2 | convolution fusion | flops 553648128 | bytes 852480 | tf_op jit(solution)/shard_map/while/body/eval_jaxpr/rfb,rs->fsb/dot_general | solution.py:77
  66.5 1.0 dynamic-slice_bitcast_fusion.2
  67.6 16.8 %fusion.20 = f32[16,32,16,256]{3,2,1,0:T(8,128)} fusion(f32[16,32,16,256]{3,2,1,0:T(8,128)} %get-tuple-element.99, s32[]{:T(128)} %get-tuple-element.98, bf16[2048,16,1]{0,1,2:T(8,128)(2,1)S(1)} %reshape.85, s32[2048,32]{0,1:T(8,128)S(1)} %dynamic-slice_bitcast_fusion.2), kind=kOutput, calls=%fused_computation.6.clone.2 | convolution fusion | flops 553648128 | bytes 852480 | tf_op jit(solution)/shard_map/while/body/eval_jaxpr/rfb,rs->fsb/dot_general | solution.py:77
  84.4 1.0 dynamic-slice_bitcast_fusion.2
  85.5 16.8 %fusion.20 = f32[16,32,16,256]{3,2,1,0:T(8,128)} fusion(f32[16,32,16,256]{3,2,1,0:T(8,128)} %get-tuple-element.99, s32[]{:T(128)} %get-tuple-element.98, bf16[2048,16,1]{0,1,2:T(8,128)(2,1)S(1)} %reshape.85, s32[2048,32]{0,1:T(8,128)S(1)} %dynamic-slice_bitcast_fusion.2), kind=kOutput, calls=%fused_computation.6.clone.2 | convolution fusion | flops 553648128 | bytes 852480 | tf_op jit(solution)/shard_map/while/body/eval_jaxpr/rfb,rs->fsb/dot_general | solution.py:77
  102.3 1.0 dynamic-slice_bitcast_fusion.2
  103.4 16.8 %fusion.20 = f32[16,32,16,256]{3,2,1,0:T(8,128)} fusion(f32[16,32,16,256]{3,2,1,0:T(8,128)} %get-tuple-element.99, s32[]{:T(128)} %get-tuple-element.98, bf16[2048,16,1]{0,1,2:T(8,128)(2,1)S(1)} %reshape.85, s32[2048,32]{0,1:T(8,128)S(1)} %dynamic-slice_bitcast_fusion.2), kind=kOutput, calls=%fused_computation.6.clone.2 | convolution fusion | flops 553648128 | bytes 852480 | tf_op jit(solution)/shard_map/while/body/eval_jaxpr/rfb,rs->fsb/dot_general | solution.py:77
  120.2 1.0 dynamic-slice_bitcast_fusion.2
  121.3 16.8 %fusion.20 = f32[16,32,16,256]{3,2,1,0:T(8,128)} fusion(f32[16,32,16,256]{3,2,1,0:T(8,128)} %get-tuple-element.99, s32[]{:T(128)} %get-tuple-element.98, bf16[2048,16,1]{0,1,2:T(8,128)(2,1)S(1)} %reshape.85, s32[2048,32]{0,1:T(8,128)S(1)} %dynamic-slice_bitcast_fusion.2), kind=kOutput, calls=%fused_computation.6.clone.2 | convolution fusion | flops 553648128 | bytes 852480 | tf_op jit(solution)/shard_map/while/body/eval_jaxpr/rfb,rs->fsb/dot_general | solution.py:77
  138.1 1.0 dynamic-slice_bitcast_fusion.2
  139.2 16.8 %fusion.20 = f32[16,32,16,256]{3,2,1,0:T(8,128)} fusion(f32[16,32,16,256]{3,2,1,0:T(8,128)} %get-tuple-element.99, s32[]{:T(128)} %get-tuple-element.98, bf16[2048,16,1]{0,1,2:T(8,128)(2,1)S(1)} %reshape.85, s32[2048,32]{0,1:T(8,128)S(1)} %dynamic-slice_bitcast_fusion.2), kind=kOutput, calls=%fused_computation.6.clone.2 | convolution fusion | flops 553648128 | bytes 852480 | tf_op jit(solution)/shard_map/while/body/eval_jaxpr/rfb,rs->fsb/dot_general | solution.py:77
  156.1 1.0 dynamic-slice_bitcast_fusion.2
  157.1 16.8 %fusion.20 = f32[16,32,16,256]{3,2,1,0:T(8,128)} fusion(f32[16,32,16,256]{3,2,1,0:T(8,128)} %get-tuple-element.99, s32[]{:T(128)} %get-tuple-element.98, bf16[2048,16,1]{0,1,2:T(8,128)(2,1)S(1)} %reshape.85, s32[2048,32]{0,1:T(8,128)S(1)} %dynamic-slice_bitcast_fusion.2), kind=kOutput, calls=%fused_computation.6.clone.2 | convolution fusion | flops 553648128 | bytes 852480 | tf_op jit(solution)/shard_map/while/body/eval_jaxpr/rfb,rs->fsb/dot_general | solution.py:77
  174.0 1.0 dynamic-slice_bitcast_fusion.2
  175.0 16.8 %fusion.20 = f32[16,32,16,256]{3,2,1,0:T(8,128)} fusion(f32[16,32,16,256]{3,2,1,0:T(8,128)} %get-tuple-element.99, s32[]{:T(128)} %get-tuple-element.98, bf16[2048,16,1]{0,1,2:T(8,128)(2,1)S(1)} %reshape.85, s32[2048,32]{0,1:T(8,128)S(1)} %dynamic-slice_bitcast_fusion.2), kind=kOutput, calls=%fused_computation.6.clone.2 | convolution fusion | flops 553648128 | bytes 852480 | tf_op jit(solution)/shard_map/while/body/eval_jaxpr/rfb,rs->fsb/dot_general | solution.py:77
  191.9 1.0 dynamic-slice_bitcast_fusion.2
  192.9 16.8 %fusion.20 = f32[16,32,16,256]{3,2,1,0:T(8,128)} fusion(f32[16,32,16,256]{3,2,1,0:T(8,128)} %get-tuple-element.99, s32[]{:T(128)} %get-tuple-element.98, bf16[2048,16,1]{0,1,2:T(8,128)(2,1)S(1)} %reshape.85, s32[2048,32]{0,1:T(8,128)S(1)} %dynamic-slice_bitcast_fusion.2), kind=kOutput, calls=%fused_computation.6.clone.2 | convolution fusion | flops 553648128 | bytes 852480 | tf_op jit(solution)/shard_map/while/body/eval_jaxpr/rfb,rs->fsb/dot_general | solution.py:77
  209.8 1.0 dynamic-slice_bitcast_fusion.2
  210.8 16.8 %fusion.20 = f32[16,32,16,256]{3,2,1,0:T(8,128)} fusion(f32[16,32,16,256]{3,2,1,0:T(8,128)} %get-tuple-element.99, s32[]{:T(128)} %get-tuple-element.98, bf16[2048,16,1]{0,1,2:T(8,128)(2,1)S(1)} %reshape.85, s32[2048,32]{0,1:T(8,128)S(1)} %dynamic-slice_bitcast_fusion.2), kind=kOutput, calls=%fused_computation.6.clone.2 | convolution fusion | flops 553648128 | bytes 852480 | tf_op jit(solution)/shard_map/while/body/eval_jaxpr/rfb,rs->fsb/dot_general | solution.py:77
  227.7 1.0 dynamic-slice_bitcast_fusion.2
  228.8 16.8 %fusion.20 = f32[16,32,16,256]{3,2,1,0:T(8,128)} fusion(f32[16,32,16,256]{3,2,1,0:T(8,128)} %get-tuple-element.99, s32[]{:T(128)} %get-tuple-element.98, bf16[2048,16,1]{0,1,2:T(8,128)(2,1)S(1)} %reshape.85, s32[2048,32]{0,1:T(8,128)S(1)} %dynamic-slice_bitcast_fusion.2), kind=kOutput, calls=%fused_computation.6.clone.2 | convolution fusion | flops 553648128 | bytes 852480 | tf_op jit(solution)/shard_map/while/body/eval_jaxpr/rfb,rs->fsb/dot_general | solution.py:77
  245.6 1.0 dynamic-slice_bitcast_fusion.2
  246.7 16.8 %fusion.20 = f32[16,32,16,256]{3,2,1,0:T(8,128)} fusion(f32[16,32,16,256]{3,2,1,0:T(8,128)} %get-tuple-element.99, s32[]{:T(128)} %get-tuple-element.98, bf16[2048,16,1]{0,1,2:T(8,128)(2,1)S(1)} %reshape.85, s32[2048,32]{0,1:T(8,128)S(1)} %dynamic-slice_bitcast_fusion.2), kind=kOutput, calls=%fused_computation.6.clone.2 | convolution fusion | flops 553648128 | bytes 852480 | tf_op jit(solution)/shard_map/while/body/eval_jaxpr/rfb,rs->fsb/dot_general | solution.py:77
  263.5 1.0 dynamic-slice_bitcast_fusion.2
  264.6 16.8 %fusion.20 = f32[16,32,16,256]{3,2,1,0:T(8,128)} fusion(f32[16,32,16,256]{3,2,1,0:T(8,128)} %get-tuple-element.99, s32[]{:T(128)} %get-tuple-element.98, bf16[2048,16,1]{0,1,2:T(8,128)(2,1)S(1)} %reshape.85, s32[2048,32]{0,1:T(8,128)S(1)} %dynamic-slice_bitcast_fusion.2), kind=kOutput, calls=%fused_computation.6.clone.2 | convolution fusion | flops 553648128 | bytes 852480 | tf_op jit(solution)/shard_map/while/body/eval_jaxpr/rfb,rs->fsb/dot_general | solution.py:77
  281.4 1.0 dynamic-slice_bitcast_fusion.2
  282.5 16.8 %fusion.20 = f32[16,32,16,256]{3,2,1,0:T(8,128)} fusion(f32[16,32,16,256]{3,2,1,0:T(8,128)} %get-tuple-element.99, s32[]{:T(128)} %get-tuple-element.98, bf16[2048,16,1]{0,1,2:T(8,128)(2,1)S(1)} %reshape.85, s32[2048,32]{0,1:T(8,128)S(1)} %dynamic-slice_bitcast_fusion.2), kind=kOutput, calls=%fused_computation.6.clone.2 | convolution fusion | flops 553648128 | bytes 852480 | tf_op jit(solution)/shard_map/while/body/eval_jaxpr/rfb,rs->fsb/dot_general | solution.py:77
  299.4 102.5 %reduce-scatter.2.cloned.1.call-done = f32[16,16,256]{2,1,0:T(8,128)} async-done(((f32[512,16,256]{2,1,0:T(8,128)}), f32[16,16,256]{2,1,0:T(8,128)}) %reduce-scatter.2.cloned.1.call-update) | async-done | bytes 262160 | tf_op jit(solution)/shard_map/reduce_scatter | solution.py:85
  401.9 39.6 %all-gather.3.cloned.1.call-done = f32[128,16,256]{2,1,0:T(8,128)} async-done(((f32[16,16,256]{2,1,0:T(8,128)}), f32[128,16,256]{2,1,0:T(8,128)}) %all-gather.3.cloned.1.call-update) | async-done | bytes 2097168 | tf_op jit(solution)/shard_map/all_gather | solution.py:15
  441.5 1.8 reduce_sum.36
  443.3 0.2 copy.24
  443.5 0.3 fusion.13
  443.8 0.2 fusion.12
  444.0 0.2 copy.20
  444.2 0.1 broadcast_divide_fusion
  444.3 0.1 multiply_reduce_fusion
  444.4 0.1 reduce_max.27
  444.5 0.1 bitcast_reduce_fusion
  444.6 18.8 %all_to_all.5 = f32[32,2,4]{2,1,0:T(2,128)S(1)} all-to-all(f32[32,2,4]{2,1,0:T(2,128)S(1)} %broadcast_in_dim.8), channel_id=1, replica_groups=mesh['rows'=8,'feat'=32] {'feat'}, dimensions={0} | all-to-all | bytes 2048 | tf_op jit(solution)/shard_map/all_to_all | solution.py:20
  463.4 0.6 reduce_max.29
  (50 shorter events, 1.4 us)
Async XLA Ops:
  7.2 5.5 %copy-start.1 = (s32[2,2048]{1,0:T(2,128)S(1)}, s32[2,2048]{1,0:T(2,128)}, u32[]{:S(2)}) copy-start(s32[2,2048]{1,0:T(2,128)} %param.8) | copy-start | bytes 49156
  7.2 5.5 %copy-start.3 = (s32[2048]{0:T(1024)S(1)}, s32[2048]{0:T(1024)}, u32[]{:S(2)}) copy-start(s32[2048]{0:T(1024)} %param.9) | copy-start | bytes 24580
  7.2 5.5 %copy-start.2 = (s32[2,2048]{1,0:T(2,128)S(1)}, s32[2,2048]{1,0:T(2,128)}, u32[]{:S(2)}) copy-start(s32[2,2048]{1,0:T(2,128)} %param.7) | copy-start | bytes 49156
  7.2 394.7 %reduce-scatter.2.cloned.1.call-start = ((), (), s32[]{:S(2)}) async-start(), calls=%async_computation.2 | async-start | bytes 8650752 | tf_op jit(solution)/shard_map/reduce_scatter | solution.py:85
  299.4 142.2 %all-gather.3.cloned.1.call-start = ((), (), s32[]{:S(2)}) async-start(), calls=%async_computation.3 | async-start | bytes 2359296 | tf_op jit(solution)/shard_map/all_gather | solution.py:15
  444.5 19.5 %copy-start = (f32[16,2,4]{0,2,1:T(4,128)}, f32[16,2,4]{0,2,1:T(4,128)S(1)}, u32[]{:S(2)}) copy-start(f32[16,2,4]{0,2,1:T(4,128)S(1)} %reduce_max.27) | copy-start | bytes 1540
Sparse Core Ops, SparseCore 0:
  299.5 102.3 reduce-scatter.1
  403.7 37.7 all-gather.2
where the time goes:
time: 472 us; the launch traced here: 471 us
  matrix products  270 us (57%)
  waiting for transfers between devices  142 us (30%)
  local copies, waits for them, and re-layouts  21.8 us (5%)
  blocking collectives  18.8 us (4%)
  between operations  14.2 us (3%)
    dot_general x16, matrix products, one_block(): jnp.einsum('rfb,rs->fsb', onehot, weights, preferred_element_type=jnp.flo...  269 us
    reduce_scatter x1, waiting for transfers between devices, on_device(): lax.psum_scatter(histogram_of(codes, weights), 'feat', scatter_dimension=...  102 us
    all_gather x1, waiting for transfers between devices, over_pieces(): return lax.all_gather(array, axis).sum(0)  39.6 us
    all_to_all x1, blocking collectives, from_everyone(): lax.all_to_all(jnp.broadcast_to(array[None], (count, *array.shape)), axis...  18.8 us
    eq x16, local copies, waits for them, and re-layouts, one_block(): onehot = (column_block[:, :, None] == bin_index).astype(jnp.bfloat16)  15.5 us
  transfers between devices with their start and end apart: 2, of which 2 were waited for; matrix products, arithmetic and copies ran while one was open for 0% of the time, Pallas kernels for 0%

commit v1 on v0

v1 whole, which is shorter than its diff:
```python
import jax
import jax.numpy as jnp
from jax import lax
from jax.experimental import pallas as pl
from jax.experimental.pallas import tpu as pltpu
from jax.sharding import PartitionSpec as P

MESH = pl.DeviceIdType.MESH
BF = jnp.bfloat16
F32 = jnp.float32
I32 = jnp.int32
Z = 8
Q = 32
SIDE = 4
STEPS = 8
TILE = 256
HIGH = lax.Precision.HIGHEST


def iota(shape, axis):
    return lax.broadcasted_iota(I32, shape, axis)


def feature_of_row(row, z, core):
    other = row >> 8
    step = (row >> 5) & 7
    a = (row >> 3) & 3
    b = (row >> 1) & 3
    even = (step & 1) == 0
    x = jnp.where(even, a, b)
    y = jnp.where(even, b, a)
    owner_core = jnp.where(other == 0, core, 1 - core)
    owner_z = (step + z + 1) & 7
    return 16 * ((y * SIDE + x) * 2 + owner_core) + 2 * owner_z + (row & 1)


def sides(hi_ref, lo_ref, weights, group, k, lane, numbers):
    upper, lower = [], []
    one, zero = jnp.ones((), BF), jnp.zeros((), BF)
    for f in range(4):
        spot = (k // 8, pl.ds(group * 4 + f, 1), pl.ds(lane, TILE))
        hi = jnp.broadcast_to(hi_ref[spot], (16, TILE)).astype(BF)
        lo = jnp.broadcast_to(lo_ref[spot], (16, TILE)).astype(BF)
        for m in range(4):
            upper.append(jnp.where(hi == numbers[m], one, zero))
        for j in range(4):
            lower.append(jnp.where(lo == jnp.asarray(j, BF), weights, zero))
    return jnp.concatenate(upper, 0), jnp.concatenate(lower, 0)


def diagonal(product):
    first = iota((64, 128), 1) < 64
    return (
        jnp.where(first, product[0:64, 0:128], product[64:128, 0:128]),
        jnp.where(first, product[128:192, 128:256], product[192:256, 128:256]),
    )


def gains(hist, z):
    row, col = iota((128, 128), 0), iota((128, 128), 1)
    half = (row >> 6) == (col >> 6)
    column = (row & 15) == (col & 15)
    upto = ((row >> 4) & 3) <= ((col >> 4) & 3)
    inside = (half & column & upto).astype(F32)
    across = (half & column).astype(F32)
    before = (iota((64, 64), 1) < iota((64, 64), 0)).astype(F32)
    earlier = jnp.dot(before, hist, precision=HIGH, preferred_element_type=F32)
    left = jnp.dot(hist, inside, precision=HIGH, preferred_element_type=F32) + jnp.dot(
        earlier, across, precision=HIGH, preferred_element_type=F32
    )
    column_sum = jnp.broadcast_to(jnp.sum(hist, axis=0, keepdims=True), (8, 128))
    total = jnp.dot(column_sum, across, precision=HIGH, preferred_element_type=F32)[0:1]
    even = (iota((64, 128), 1) & 1) == 0

    def both(v):
        return v + jnp.where(even, pltpu.roll(v, 127, 1), pltpu.roll(v, 1, 1))

    total = jnp.broadcast_to(total, (64, 128))
    n_left = both(left)
    n_total = both(total)
    n_right = n_total - n_left
    frac = n_left / jnp.maximum(n_total, 1.0)
    terms = (left - total * frac) ** 2
    scaled = n_total / (jnp.maximum(n_left, 1.0) * jnp.maximum(n_right, 1.0))
    best = jnp.max(both(terms * scaled), axis=0, keepdims=True)
    best = jnp.broadcast_to(best, (8, 128))
    best = jnp.maximum(best, pltpu.roll(best, 112, 1))
    best = jnp.maximum(best, pltpu.roll(best, 96, 1))
    node, lane = iota((8, 128), 0), iota((8, 128), 1)
    picked = jnp.where((lane & 63) == 2 * node, best, 0.0)
    place = ((row >> 6) == (col & 1)) & ((col >> 1) == z)
    return jnp.dot(picked, place.astype(F32), precision=HIGH, preferred_element_type=F32)


def kernel(
    codes_ref,
    node_ref,
    bag_ref,
    label_ref,
    feature_ref,
    best_ref,
    hi_ref,
    lo_ref,
    codes_out,
    codes_in,
    weight_ref,
    weight_out,
    weight_in,
    hist,
    a1_in,
    a2_in,
    b1_in,
    b2_in,
    z_in,
    own_gain,
    gain_in,
    own_best,
    best_in,
    c_send,
    c_recv,
    ab_send,
    ab_recv,
    z_send,
    z_recv,
    g_send,
    g_recv,
    n_send,
    n_recv,
):
    z = lax.axis_index("rows")
    q = lax.axis_index("feat")
    core = lax.rem(q, 2)
    x = lax.rem(q // 2, SIDE)
    y = q // 8
    barrier = pltpu.get_barrier_semaphore()

    def greet_plane(i, carry):
        pl.semaphore_signal(
            barrier, inc=1, device_id=(z, lax.rem(q + i, Q)), device_id_type=MESH
        )
        return carry

    def greet_column(i, carry):
        pl.semaphore_signal(
            barrier, inc=1, device_id=(lax.rem(z + i, Z), q), device_id_type=MESH
        )
        return carry

    lax.fori_loop(1, Q, greet_plane, 0)
    lax.fori_loop(1, Z, greet_column, 0)

    rows = label_ref.shape[1]
    number = iota((8, rows), 0)
    parts = []
    for tree in range(2):
        key = node_ref[tree : tree + 1, :] * 2 + label_ref[...]
        bag = jnp.broadcast_to(bag_ref[tree : tree + 1, :], (8, rows))
        parts.append(jnp.where(jnp.broadcast_to(key, (8, rows)) == number, bag, 0).astype(F32))
    weight = jnp.concatenate(parts, 0)
    weight_out[...] = weight
    weight_ref[0] = weight.astype(BF)

    wanted = feature_of_row(iota((512, 512), 0), z, core)
    order = (wanted == iota((512, 512), 1)).astype(F32).astype(BF)

    def split(table):
        hi = jnp.floor(table * 0.25)
        return hi, table - 4.0 * hi

    def arrange(k, carry):
        start = pl.multiple_of(k * TILE, TILE)
        block = codes_ref[pl.ds(start, TILE), :].astype(F32).astype(BF)
        table = lax.dot_general(
            order, block, (((1,), (1,)), ((), ())), preferred_element_type=F32
        )
        hi, lo = split(table[:256])
        hi_ref[0, :, pl.ds(start, TILE)] = hi
        lo_ref[0, :, pl.ds(start, TILE)] = lo
        codes_out[:, pl.ds(start, TILE)] = table[256:]
        return carry

    lax.fori_loop(0, rows // TILE, arrange, 0)

    partner = (z, q + 1 - 2 * core)

    def code_copy(t):
        piece = pl.ds(pl.multiple_of(t * 32, 32), 32)
        return pltpu.make_async_remote_copy(
            codes_out.at[piece], codes_in.at[piece], c_send.at[t], c_recv.at[t],
            device_id=partner, device_id_type=MESH,
        )

    weight_copy = pltpu.make_async_remote_copy(
        weight_out, weight_in, c_send.at[STEPS], c_recv.at[STEPS],
        device_id=partner, device_id_type=MESH,
    )
    pl.semaphore_wait(barrier, Q - 1 + Z - 1)
    weight_copy.start()

    def send_codes(t, carry):
        code_copy(t).start()
        return carry

    lax.fori_loop(0, STEPS, send_codes, 0)
    weight_copy.wait_recv()
    weight_ref[1] = weight_in[...].astype(BF)

    def near(t, axis, way):
        on_y = lax.rem(t + axis, 2)
        on_x = 1 - on_y
        nx = lax.rem(x + on_x * way + SIDE, SIDE)
        ny = lax.rem(y + on_y * way + SIDE, SIDE)
        return (z, (ny * SIDE + nx) * 2 + core)

    def spot(t, axis, shift):
        on_y = lax.rem(t + axis, 2)
        here = on_y * y + (1 - on_y) * x
        return lax.rem(here + shift + SIDE, SIDE)

    def remote(t, kind, side, src, dst, device):
        return pltpu.make_async_remote_copy(
            src, dst, ab_send.at[t, kind, side], ab_recv.at[t, kind, side],
            device_id=device, device_id_type=MESH,
        )

    def copies_a(t, kind):
        right, left = near(t, 0, 1), near(t, 0, -1)
        if kind == 0:
            far = spot(t, 0, 2) * 4
            return (
                remote(t, 0, 0, hist.at[t, pl.ds(far, 2)], a1_in.at[t, 0], right),
                remote(t, 0, 1, hist.at[t, pl.ds(far + 2, 2)], a1_in.at[t, 1], left),
            )
        r, l = spot(t, 0, 1) * 4, spot(t, 0, -1) * 4
        first, second = (2, 0) if kind == 1 else (0, 2)
        return (
            remote(t, kind, 0, hist.at[t, pl.ds(r + first, 2)],
                   a2_in.at[t, 0, pl.ds(first, 2)], right),
            remote(t, kind, 1, hist.at[t, pl.ds(l + second, 2)],
                   a2_in.at[t, 1, pl.ds(second, 2)], left),
        )

    def copies_b(t, kind):
        right, left = near(t, 1, 1), near(t, 1, -1)
        base = spot(t, 0, 0) * 4
        top, low = pl.ds(0, 32), pl.ds(32, 32)
        if kind == 0:
            far = base + spot(t, 1, 2)
            return (
                remote(t, 3, 0, hist.at[t, far, top], b1_in.at[t, 0], right),
                remote(t, 3, 1, hist.at[t, far, low], b1_in.at[t, 1], left),
            )
        r, l = base + spot(t, 1, 1), base + spot(t, 1, -1)
        first, second = (low, top) if kind == 1 else (top, low)
        return (
            remote(t, 3 + kind, 0, hist.at[t, r, first], b2_in.at[t, 0, first], right),
            remote(t, 3 + kind, 1, hist.at[t, l, second], b2_in.at[t, 1, second], left),
        )

    def start(copies):
        for copy in copies:
            copy.start()

    def arrived(copies):
        for copy in copies:
            copy.wait_recv()

    def a1(t):
        start(copies_a(t, 0))
        start(copies_a(t, 1))

    def a2(t):
        arrived(copies_a(t, 0))
        r, l = spot(t, 0, 1) * 4, spot(t, 0, -1) * 4
        hist[t, pl.ds(r, 2)] = hist[t, pl.ds(r, 2)] + a1_in[t, 0]
        hist[t, pl.ds(l + 2, 2)] = hist[t, pl.ds(l + 2, 2)] + a1_in[t, 1]
        start(copies_a(t, 2))

    def b1(t):
        arrived(copies_a(t, 1))
        arrived(copies_a(t, 2))
        mine = pl.ds(spot(t, 0, 0) * 4, 4)
        hist[t, mine] = hist[t, mine] + (a2_in[t, 0] + a2_in[t, 1])
        start(copies_b(t, 0))
        start(copies_b(t, 1))

    def b2(t):
        arrived(copies_b(t, 0))
        base = spot(t, 0, 0) * 4
        r, l = base + spot(t, 1, 1), base + spot(t, 1, -1)
        hist[t, r, 0:32] = hist[t, r, 0:32] + b1_in[t, 0]
        hist[t, l, 32:64] = hist[t, l, 32:64] + b1_in[t, 1]
        start(copies_b(t, 2))

    def plane_sum(t):
        arrived(copies_b(t, 1))
        arrived(copies_b(t, 2))
        mine = spot(t, 0, 0) * 4 + spot(t, 1, 0)
        return mine, hist[t, mine] + (b2_in[t, 0] + b2_in[t, 1])

    def z_copy(t):
        mine = spot(t, 0, 0) * 4 + spot(t, 1, 0)
        return pltpu.make_async_remote_copy(
            hist.at[t, mine], z_in.at[t], z_send.at[t], z_recv.at[t],
            device_id=(lax.rem(z + 1 + t, Z), q), device_id_type=MESH,
        )

    def to_owner(t):
        mine, value = plane_sum(t)
        hist[t, mine] = value
        z_copy(t).start()

    count = iota((16, TILE), 0).astype(F32)
    numbers = [(count + 16.0 * m).astype(BF) for m in range(4)]

    def histogram(t, begin, end):
        def some(i, carry):
            for u in range(2):
                group = i * 2 + u
                total = None
                for k in range(16):
                    lane = (k % 8) * TILE
                    upper, lower = sides(
                        hi_ref, lo_ref, weight_ref[k // 8, :, lane : lane + TILE],
                        t * 8 + group, k, lane, numbers,
                    )
                    part = lax.dot_general(
                        upper, lower, (((1,), (1,)), ((), ())), preferred_element_type=F32
                    )
                    total = part if total is None else total + part
                hist[t, group * 2], hist[t, group * 2 + 1] = diagonal(total)
            return carry

        lax.fori_loop(begin, end, some, 0)

    def step(t, carry):
        code_copy(t).wait_recv()
        piece = pl.ds(pl.multiple_of(t * 32, 32), 32)
        hi, lo = split(codes_in[piece])
        hi_ref[1, piece] = hi
        lo_ref[1, piece] = lo
        histogram(t, 0, 2)
        pl.when(t >= 3)(lambda: to_owner(t - 3))
        pl.when(t >= 2)(lambda: b1(t - 2))
        pl.when(t >= 1)(lambda: a2(t - 1))
        histogram(t, 2, 4)
        pl.when(t >= 2)(lambda: b2(t - 2))
        a1(t)
        return carry

    lax.fori_loop(0, STEPS, step, 0)
    last = STEPS - 1
    to_owner(last - 2)
    b1(last - 1)
    a2(last)
    b2(last - 1)
    to_owner(last - 1)
    b1(last)
    b2(last)
    _, summed = plane_sum(last)
    for t in range(STEPS - 1):
        z_copy(t).wait_recv()
    summed = summed + jnp.sum(z_in[...], axis=0)

    own_gain[...] = gains(summed, z)

    def gain_copy(i):
        return pltpu.make_async_remote_copy(
            own_gain, gain_in.at[i - 1], g_send.at[i - 1], g_recv.at[i - 1],
            device_id=(lax.rem(z + i, Z), q), device_id_type=MESH,
        )

    def best_copy(i):
        return pltpu.make_async_remote_copy(
            own_best, best_in.at[i - 1], n_send.at[i - 1], n_recv.at[i - 1],
            device_id=(z, lax.rem(q + i, Q)), device_id_type=MESH,
        )

    def loop(first, end, act):
        def body(i, carry):
            act(i)
            return carry

        lax.fori_loop(first, end, body, 0)

    loop(1, Z, lambda i: gain_copy(i).start())
    loop(1, Z, lambda i: gain_copy(i).wait_recv())
    together = own_gain[...] + jnp.sum(gain_in[...], axis=0)
    feature_ref[...] = together
    own_best[...] = jnp.broadcast_to(jnp.max(together, axis=1, keepdims=True), (8, 128))
    loop(1, Q, lambda i: best_copy(i).start())

    weight_copy.wait_send()

    def leave(t):
        code_copy(t).wait_send()
        for kind in range(3):
            for copy in (*copies_a(t, kind), *copies_b(t, kind)):
                copy.wait_send()

    loop(0, STEPS, leave)
    loop(0, STEPS - 1, lambda t: z_copy(t).wait_send())
    loop(1, Z, lambda i: gain_copy(i).wait_send())
    loop(1, Q, lambda i: best_copy(i).wait_recv())
    best_ref[...] = jnp.maximum(own_best[...], jnp.max(best_in[...], axis=0))
    loop(1, Q, lambda i: best_copy(i).wait_send())


def on_device(codes, node_ids, bag_counts, labels):
    rows, features = codes.shape
    dma = pltpu.SemaphoreType.DMA
    feature_gain, node_gain = pl.pallas_call(
        kernel,
        out_shape=[jax.ShapeDtypeStruct((8, 128), F32)] * 2,
        in_specs=[pl.BlockSpec(memory_space=pltpu.VMEM)] * 4,
        out_specs=[pl.BlockSpec(memory_space=pltpu.VMEM)] * 2,
        scratch_shapes=[
            pltpu.VMEM((2, 256, rows), F32),
            pltpu.VMEM((2, 256, rows), F32),
            pltpu.VMEM((256, rows), F32),
            pltpu.VMEM((256, rows), F32),
            pltpu.VMEM((2, 16, rows), BF),
            pltpu.VMEM((16, rows), F32),
            pltpu.VMEM((16, rows), F32),
            pltpu.VMEM((STEPS, 16, 64, 128), F32),
            pltpu.VMEM((STEPS, 2, 2, 64, 128), F32),
            pltpu.VMEM((STEPS, 2, 4, 64, 128), F32),
            pltpu.VMEM((STEPS, 2, 32, 128), F32),
            pltpu.VMEM((STEPS, 2, 64, 128), F32),
            pltpu.VMEM((STEPS - 1, 64, 128), F32),
            pltpu.VMEM((8, 128), F32),
            pltpu.VMEM((Z - 1, 8, 128), F32),
            pltpu.VMEM((8, 128), F32),
            pltpu.VMEM((Q - 1, 8, 128), F32),
            dma((STEPS + 1,)),
            dma((STEPS + 1,)),
            dma((STEPS, 6, 2)),
            dma((STEPS, 6, 2)),
            dma((STEPS - 1,)),
            dma((STEPS - 1,)),
            dma((Z - 1,)),
            dma((Z - 1,)),
            dma((Q - 1,)),
            dma((Q - 1,)),
        ],
        compiler_params=pltpu.CompilerParams(
            collective_id=0, has_side_effects=True, vmem_limit_bytes=60 * 1024 * 1024
        ),
    )(codes, node_ids, bag_counts, labels.reshape(1, rows))
    return feature_gain[:, :16].reshape(2, 4, 16), node_gain[:, 0].reshape(2, 4)


def solution(mesh):
    return jax.shard_map(
        on_device,
        mesh=mesh,
        in_specs=(
            P(("rows", "feat"), None),
            P(None, ("rows", "feat")),
            P(None, ("rows", "feat")),
            P(("rows", "feat")),
        ),
        out_specs=(P(None, None, "feat"), P()),
        check_vma=False,
    )
```

time: 472 us -> 102 us (0.22)
  matrix products: 270 us -> 0 us
  waiting for transfers between devices: 142 us -> 0 us
  Pallas kernels: 0 us -> 98.6 us
  local copies, waits for them, and re-layouts: 21.8 us -> 2.71 us
  blocking collectives: 18.8 us -> 0 us
  between operations: 14.2 us -> 0.64 us
    dot_general x17 -> x0, matrix products: 270 us -> none  [the longest x16 269 us: one_block(): jnp.einsum('rfb,rs->fsb', onehot, weights, preferred_element_type=jnp.flo...]
    reduce_scatter x1 -> x0, waiting for transfers between devices: 102 us -> none  [on_device(): lax.psum_scatter(histogram_of(codes, weights), 'feat', scatter_dimension=...]
    pallas_call x0 -> x1, Pallas kernels: none -> 98.6 us  [on_device(): pl.pallas_call(kernel, out_shape=[jax.ShapeDtypeStruct((8, 128), F32)] *...]
    all_gather x1 -> x0, waiting for transfers between devices: 39.6 us -> none  [over_pieces(): return lax.all_gather(array, axis).sum(0)]
    all_to_all x1 -> x0, blocking collectives: 18.8 us -> none  [from_everyone(): lax.all_to_all(jnp.broadcast_to(array[None], (count, *array.shape)), axis...]
    eq x16 -> x0, local copies, waits for them, and re-layouts: 15.5 us -> none  [one_block(): onehot = (column_block[:, :, None] == bin_index).astype(jnp.bfloat16)]
  transfers between devices with their start and end apart: 2 -> 0, of which waited for: 2 -> 0; matrix products, arithmetic and copies ran while one was open for 0% -> 0% of each run, Pallas kernels for 0% -> 0%
where the time goes in v1:
time: 102 us
  Pallas kernels  98.6 us (97%)
  local copies, waits for them, and re-layouts  2.71 us (3%)
    pallas_call x1, Pallas kernels, on_device(): pl.pallas_call(kernel, out_shape=[jax.ShapeDtypeStruct((8, 128), F32)] *...  98.6 us

profile of v1, /device:TPU:1, one launch (start us, length us, event | category | flops | bytes accessed | tf_op | source)
XLA Modules:
  0.0 101.9 jit_solution(17595200630889667045)
XLA Ops:
  0.6 98.6 %shard_map.59 = (f32[8,128]{1,0:T(8,128)}, f32[8,128]{1,0:T(8,128)}) custom-call(s32[2048,512]{1,0:T(8,128)} %codes_ref.1, s32[2,2048]{1,0:T(2,128)} %node_ref.1, s32[2,2048]{1,0:T(2,128)} %bag_ref.1, s32[1,2048]{1,0:T(1,128)} %bitcast.3), custom_call_target="tpu_custom_call" | custom-call | tf_op jit(solution)/shard_map/pallas_call | solution.py:412
  99.2 0.8 slice_reduce_fusion
  100.0 0.6 reshape_squeeze.3
  100.7 1.3 %copy.7 = f32[2,4,16]{2,1,0:T(4,128)} copy(f32[2,4,16]{2,1,0:T(4,128)} %bitcast.4) | data formatting | bytes 1024

commit v2 on v0

v2 whole, which is shorter than its diff:
```python
import jax
import jax.numpy as jnp
from jax import lax
from jax.experimental import pallas as pl
from jax.experimental.pallas import tpu as pltpu
from jax.sharding import PartitionSpec as P

MESH = pl.DeviceIdType.MESH
BF = jnp.bfloat16
F32 = jnp.float32
I32 = jnp.int32
F8 = jnp.float8_e4m3fn
Z = 8
Q = 32
SIDE = 4
STEPS = 8
TILE = 256
LOAD = 512
SCALE = 4096.0
HIGH = lax.Precision.HIGHEST


def iota(shape, axis):
    return lax.broadcasted_iota(I32, shape, axis)


def feature_of_row(row, z, core):
    other = row >> 8
    step = (row >> 5) & 7
    a = (row >> 3) & 3
    b = (row >> 1) & 3
    even = (step & 1) == 0
    x = jnp.where(even, a, b)
    y = jnp.where(even, b, a)
    owner_core = jnp.where(other == 0, core, 1 - core)
    owner_z = (step + z + 1) & 7
    return 16 * ((y * SIDE + x) * 2 + owner_core) + 2 * owner_z + (row & 1)


def sides(hi_ref, lo_ref, weights, scale, source, row, lane, numbers, quads):
    upper, lower = [], []
    zero, nothing = jnp.zeros((), BF), jnp.zeros((32, TILE), F8)
    for f in range(4):
        spot = (source, pl.ds(row + f, 1), pl.ds(lane, TILE))
        hi = jnp.broadcast_to(hi_ref[spot], (16, TILE)).astype(BF)
        lo = jnp.broadcast_to(lo_ref[spot], (32, TILE)).astype(BF)
        for m in range(2):
            upper.append(jnp.where(hi == numbers[m], scale, zero))
        for m in range(2):
            lower.append(jnp.where(lo == quads[m], weights, nothing))
    return jnp.concatenate(upper, 0), jnp.concatenate(lower, 0)


def diagonal(product):
    first = iota((32, 128), 1) < 64
    return (
        jnp.where(first, product[0:32, 0:128], product[32:64, 0:128]),
        jnp.where(first, product[64:96, 128:256], product[96:128, 128:256]),
    )


def classes(product):
    out = []
    for both in diagonal(product):
        second = jnp.floor(both * (1.0 / SCALE))
        out += [both - SCALE * second, second]
    return out


def gains(hist, z):
    row, col = iota((128, 128), 0), iota((128, 128), 1)
    half = (row >> 6) == (col >> 6)
    column = (row & 7) == (col & 7)
    upto = ((row >> 3) & 7) <= ((col >> 3) & 7)
    inside = (half & column & upto).astype(F32)
    across = (half & column).astype(F32)
    here, there = iota((64, 64), 0), iota((64, 64), 1)
    before = ((there < here) & ((there >> 5) == (here >> 5))).astype(F32)
    earlier = jnp.dot(before, hist, precision=HIGH, preferred_element_type=F32)
    left = jnp.dot(hist, inside, precision=HIGH, preferred_element_type=F32) + jnp.dot(
        earlier, across, precision=HIGH, preferred_element_type=F32
    )
    sums = jnp.concatenate(
        [
            jnp.broadcast_to(jnp.sum(hist[32 * c : 32 * c + 32], axis=0, keepdims=True), (8, 128))
            for c in range(2)
        ],
        0,
    )
    sums = jnp.dot(sums, across, precision=HIGH, preferred_element_type=F32)
    total = [jnp.broadcast_to(sums[8 * c : 8 * c + 1], (32, 128)) for c in range(2)]
    left = [left[:32], left[32:]]
    n_left = left[0] + left[1]
    n_total = total[0] + total[1]
    n_right = n_total - n_left
    frac = n_left / jnp.maximum(n_total, 1.0)
    scaled = n_total / (jnp.maximum(n_left, 1.0) * jnp.maximum(n_right, 1.0))
    spread = [(left[c] - total[c] * frac) ** 2 * scaled for c in range(2)]
    best = jnp.max(spread[0] + spread[1], axis=0, keepdims=True)
    best = jnp.broadcast_to(best, (8, 128))
    for shift in (8, 16, 32):
        best = jnp.maximum(best, pltpu.roll(best, 128 - shift, 1))
    node, lane = iota((8, 128), 0), iota((8, 128), 1)
    picked = jnp.where((lane & 63) == node, best, 0.0)
    place = ((row >> 6) == (col & 1)) & ((col >> 1) == z)
    return jnp.dot(picked, place.astype(F32), precision=HIGH, preferred_element_type=F32)


def kernel(
    codes_hbm,
    node_hbm,
    bag_hbm,
    label_hbm,
    feature_ref,
    best_ref,
    codes_ref,
    node_ref,
    bag_ref,
    label_ref,
    hi_ref,
    lo_ref,
    codes_out,
    codes_in,
    weight_ref,
    scale_ref,
    weight_out,
    weight_in,
    hist,
    a1_in,
    a2_in,
    b_in,
    z_in,
    own_gain,
    gain_in,
    own_best,
    best_in,
    load_sem,
    code_sent,
    weight_sent,
    block_sent,
    gain_sent,
    best_sent,
    code_came,
    weight_came,
    block_came,
    z_came,
    gain_came,
    best_came,
):
    rows = codes_hbm.shape[0]
    z = lax.axis_index("rows")
    q = lax.axis_index("feat")
    core = lax.rem(q, 2)
    x = lax.rem(q // 2, SIDE)
    y = q // 8
    barrier = pltpu.get_barrier_semaphore()

    def loop(first, end, act):
        def body(i, carry):
            act(i)
            return carry

        lax.fori_loop(first, end, body, 0)

    def arrived(ref, sem):
        pltpu.make_async_copy(ref, ref, sem).wait()

    pieces = rows // LOAD
    small = [
        pltpu.make_async_copy(node_hbm, node_ref, load_sem.at[pieces]),
        pltpu.make_async_copy(bag_hbm, bag_ref, load_sem.at[pieces + 1]),
        pltpu.make_async_copy(label_hbm, label_ref, load_sem.at[pieces + 2]),
    ]

    def load(k):
        piece = pl.ds(pl.multiple_of(k * LOAD, LOAD), LOAD)
        return pltpu.make_async_copy(codes_hbm.at[piece], codes_ref.at[piece], load_sem.at[k])

    def greet(z, q):
        pl.semaphore_signal(barrier, inc=1, device_id=(z, q), device_id_type=MESH)

    for copy in small:
        copy.start()
    loop(0, pieces, lambda k: load(k).start())
    loop(1, Z, lambda i: greet(lax.rem(z + i, Z), q))
    loop(1, Q, lambda i: greet(z, lax.rem(q + i, Q)))

    wanted = feature_of_row(iota((512, 512), 0), z, core)
    order = (wanted == iota((512, 512), 1)).astype(F32).astype(BF)

    for copy in small:
        copy.wait()
    number = iota((4, rows), 0)
    parts = []
    for tree in range(2):
        node = jnp.broadcast_to(node_ref[tree : tree + 1, :], (4, rows))
        bag = jnp.broadcast_to(bag_ref[tree : tree + 1, :], (4, rows))
        parts.append(jnp.where(node == number, bag, 0).astype(F32))
    weight = jnp.concatenate(parts, 0)
    scale = jnp.where(jnp.broadcast_to(label_ref[...], (8, rows)) == 1, SCALE, 1.0)
    weight_out[:8] = weight
    weight_out[8:] = scale

    def keep_weights(source, weight, scale):
        weight_ref[source] = jnp.concatenate([weight] * 4, 0).astype(BF).astype(F8)
        scale_ref[source] = jnp.concatenate([scale] * 2, 0).astype(BF)

    keep_weights(0, weight, scale)

    def split(table):
        hi = jnp.floor(table * 0.125)
        return hi, table - 8.0 * hi

    def arrange(k):
        load(k).wait()
        part = pl.ds(pl.multiple_of(k * LOAD, LOAD), LOAD)
        table = lax.dot_general(
            order, codes_ref[part, :].astype(F32).astype(BF), (((1,), (1,)), ((), ())),
            preferred_element_type=F32,
        )
        hi, lo = split(table[:256])
        hi_ref[0, :, part] = hi
        lo_ref[0, :, part] = lo
        codes_out[:, part] = table[256:]

    loop(0, pieces, arrange)

    partner = (z, q + 1 - 2 * core)

    def send_codes(t):
        piece = pl.ds(pl.multiple_of(t * 32, 32), 32)
        pltpu.make_async_remote_copy(
            codes_out.at[piece], codes_in.at[piece], code_sent, code_came.at[t],
            device_id=partner, device_id_type=MESH,
        ).start()

    pl.semaphore_wait(barrier, Q - 1 + Z - 1)
    pltpu.make_async_remote_copy(
        weight_out, weight_in, weight_sent, weight_came,
        device_id=partner, device_id_type=MESH,
    ).start()
    loop(0, STEPS, send_codes)
    arrived(weight_in, weight_came)
    keep_weights(1, weight_in[:8], weight_in[8:])

    def near(t, axis, way):
        on_y = lax.rem(t + axis, 2)
        on_x = 1 - on_y
        nx = lax.rem(x + on_x * way + SIDE, SIDE)
        ny = lax.rem(y + on_y * way + SIDE, SIDE)
        return (z, (ny * SIDE + nx) * 2 + core)

    def spot(t, axis, shift):
        on_y = lax.rem(t + axis, 2)
        here = on_y * y + (1 - on_y) * x
        return lax.rem(here + shift + SIDE, SIDE)

    def block(t, a, b=0):
        return t * 16 + a * 4 + b

    def send(t, stage, src, dst, device):
        pltpu.make_async_remote_copy(
            src, dst, block_sent, block_came.at[t, stage],
            device_id=device, device_id_type=MESH,
        ).start()

    def two(first):
        return pl.ds(first, 2)

    def a1(t):
        right, left = near(t, 0, 1), near(t, 0, -1)
        far, r, l = (block(t, spot(t, 0, shift)) for shift in (2, 1, -1))
        send(t, 0, hist.at[two(far)], a1_in.at[t, 0], right)
        send(t, 0, hist.at[two(far + 2)], a1_in.at[t, 1], left)
        send(t, 1, hist.at[two(r + 2)], a2_in.at[t, 0, two(2)], right)
        send(t, 1, hist.at[two(l)], a2_in.at[t, 1, two(0)], left)

    def a2(t):
        arrived(a1_in.at[t], block_came.at[t, 0])
        r, l = block(t, spot(t, 0, 1)), block(t, spot(t, 0, -1))
        hist[two(r)] = hist[two(r)] + a1_in[t, 0]
        hist[two(l + 2)] = hist[two(l + 2)] + a1_in[t, 1]
        send(t, 1, hist.at[two(r)], a2_in.at[t, 0, two(0)], near(t, 0, 1))
        send(t, 1, hist.at[two(l + 2)], a2_in.at[t, 1, two(2)], near(t, 0, -1))

    def b1(t):
        arrived(a2_in.at[t], block_came.at[t, 1])
        first = block(t, spot(t, 0, 0))
        mine = pl.ds(first, 4)
        hist[mine] = hist[mine] + (a2_in[t, 0] + a2_in[t, 1])
        for i, shift in enumerate((2, 1, -1)):
            send(t, 2, hist.at[first + spot(t, 1, shift)], b_in.at[t, i], near(t, 1, shift))

    def plane_sum(t):
        arrived(b_in.at[t], block_came.at[t, 2])
        mine = block(t, spot(t, 0, 0), spot(t, 1, 0))
        return mine, (hist[mine] + b_in[t, 0]) + (b_in[t, 1] + b_in[t, 2])

    def to_owner(t):
        mine, value = plane_sum(t)
        hist[mine] = value
        pltpu.make_async_remote_copy(
            hist.at[mine], z_in.at[t], block_sent, z_came,
            device_id=(lax.rem(z + 1 + t, Z), q), device_id_type=MESH,
        ).start()

    count = iota((16, TILE), 0).astype(F32)
    numbers = [(count + 16.0 * m).astype(BF) for m in range(2)]
    count = (iota((32, TILE), 0) >> 3).astype(F32)
    quads = [(count + 4.0 * m).astype(BF) for m in range(2)]
    passes = 2 * rows // TILE
    span = 1024 // TILE

    def histogram(t, begin, end):
        def some(i):
            for u in range(2):
                group = t * 8 + i * 2 + u
                counts = None
                for first in range(0, passes, span):
                    total = None
                    for k in range(first, first + span):
                        source, lane = divmod(k * TILE, rows)
                        cols = slice(lane, lane + TILE)
                        upper, lower = sides(
                            hi_ref, lo_ref, weight_ref[source, :, cols],
                            scale_ref[source, :, cols], source, group * 4, lane, numbers, quads,
                        )
                        part = lax.dot_general(
                            upper, lower, (((1,), (1,)), ((), ())), preferred_element_type=F32
                        )
                        total = part if total is None else total + part
                    more = classes(total)
                    counts = more if counts is None else [a + b for a, b in zip(counts, more)]
                for e in range(2):
                    hist[group * 2 + e, 0:32] = counts[2 * e]
                    hist[group * 2 + e, 32:64] = counts[2 * e + 1]

        loop(begin, end, some)

    def step(t):
        piece = pl.ds(pl.multiple_of(t * 32, 32), 32)
        arrived(codes_in.at[piece], code_came.at[t])
        hi, lo = split(codes_in[piece])
        hi_ref[1, piece] = hi
        lo_ref[1, piece] = lo
        histogram(t, 0, 2)
        pl.when(t >= 2)(lambda: a2(t - 2))
        pl.when(t >= 5)(lambda: to_owner(t - 5))
        histogram(t, 2, 4)
        a1(t)
        pl.when(t >= 3)(lambda: b1(t - 3))

    loop(0, STEPS, step)
    last = STEPS - 1
    a2(last - 1)
    to_owner(last - 4)
    b1(last - 2)
    a2(last)
    to_owner(last - 3)
    b1(last - 1)
    to_owner(last - 2)
    b1(last)
    to_owner(last - 1)
    _, summed = plane_sum(last)
    arrived(z_in, z_came)
    summed = summed + jnp.sum(z_in[...], axis=0)
    own_gain[...] = gains(summed, z)

    def send_gain(i):
        pltpu.make_async_remote_copy(
            own_gain, gain_in.at[i - 1], gain_sent, gain_came,
            device_id=(lax.rem(z + i, Z), q), device_id_type=MESH,
        ).start()

    def send_best(i):
        pltpu.make_async_remote_copy(
            own_best, best_in.at[i - 1], best_sent, best_came,
            device_id=(z, lax.rem(q + i, Q)), device_id_type=MESH,
        ).start()

    loop(1, Z, send_gain)
    arrived(gain_in, gain_came)
    together = own_gain[...] + jnp.sum(gain_in[...], axis=0)
    own_best[...] = jnp.broadcast_to(jnp.max(together, axis=1, keepdims=True), (8, 128))
    loop(1, Q, send_best)
    for tree in range(2):
        feature_ref[tree] = together[4 * tree : 4 * tree + 4, :16]

    arrived(weight_out, weight_sent)
    arrived(codes_out, code_sent)
    arrived(hist.at[pl.ds(0, STEPS * 16 - 1)], block_sent)
    arrived(gain_in, gain_sent)
    arrived(best_in, best_came)
    best = jnp.maximum(own_best[...], jnp.max(best_in[...], axis=0))
    for tree in range(2):
        chosen = iota((8, 128), 0) == iota((8, 128), 1) + 4 * tree
        line = jnp.sum(jnp.where(chosen, best, 0.0), axis=0, keepdims=True)
        best_ref[tree : tree + 1, :] = line[:, :4]
    arrived(best_in, best_sent)


def hand_over(feature_in, best_in, feature_ref, best_ref):
    feature_ref[...] = feature_in[...]
    best_ref[...] = best_in[...]


def on_device(codes, node_ids, bag_counts, labels):
    rows, features = codes.shape
    dma = pltpu.SemaphoreType.DMA
    whole = pl.BlockSpec(memory_space=pltpu.VMEM)
    outs = [jax.ShapeDtypeStruct((2, 4, 16), F32), jax.ShapeDtypeStruct((2, 4), F32)]
    results = pl.pallas_call(
        kernel,
        out_shape=outs,
        in_specs=[pl.BlockSpec(memory_space=pl.ANY)] * 4,
        out_specs=[whole] * 2,
        scratch_shapes=[
            pltpu.VMEM((rows, features), I32),
            pltpu.VMEM((2, rows), I32),
            pltpu.VMEM((2, rows), I32),
            pltpu.VMEM((1, rows), I32),
            pltpu.VMEM((2, 256, rows), F32),
            pltpu.VMEM((2, 256, rows), F32),
            pltpu.VMEM((256, rows), F32),
            pltpu.VMEM((256, rows), F32),
            pltpu.VMEM((2, 32, rows), F8),
            pltpu.VMEM((2, 16, rows), BF),
            pltpu.VMEM((16, rows), F32),
            pltpu.VMEM((16, rows), F32),
            pltpu.VMEM((STEPS * 16, 64, 128), F32),
            pltpu.VMEM((STEPS, 2, 2, 64, 128), F32),
            pltpu.VMEM((STEPS, 2, 4, 64, 128), F32),
            pltpu.VMEM((STEPS, 3, 64, 128), F32),
            pltpu.VMEM((STEPS - 1, 64, 128), F32),
            pltpu.VMEM((8, 128), F32),
            pltpu.VMEM((Z - 1, 8, 128), F32),
            pltpu.VMEM((8, 128), F32),
            pltpu.VMEM((Q - 1, 8, 128), F32),
            dma((rows // LOAD + 3,)),
            dma(()),
            dma(()),
            dma(()),
            dma(()),
            dma(()),
            dma((STEPS,)),
            dma(()),
            dma((STEPS, 3)),
            dma(()),
            dma(()),
            dma(()),
        ],
        compiler_params=pltpu.CompilerParams(
            collective_id=0, has_side_effects=True, vmem_limit_bytes=60 * 1024 * 1024
        ),
    )(codes, node_ids, bag_counts, labels.reshape(1, rows))
    return pl.pallas_call(
        hand_over, out_shape=outs, in_specs=[whole] * 2, out_specs=[whole] * 2
    )(*results)


def solution(mesh):
    return jax.shard_map(
        on_device,
        mesh=mesh,
        in_specs=(
            P(("rows", "feat"), None),
            P(None, ("rows", "feat")),
            P(None, ("rows", "feat")),
            P(("rows", "feat")),
        ),
        out_specs=(P(None, None, "feat"), P()),
        check_vma=False,
    )
```

time: 472 us -> 68.9 us (0.15)
  matrix products: 270 us -> 0 us
  waiting for transfers between devices: 142 us -> 0 us
  Pallas kernels: 0 us -> 68.1 us
  local copies, waits for them, and re-layouts: 21.8 us -> 0 us
  blocking collectives: 18.8 us -> 0 us
  between operations: 14.2 us -> 0.64 us
    dot_general x17 -> x0, matrix products: 270 us -> none  [the longest x16 269 us: one_block(): jnp.einsum('rfb,rs->fsb', onehot, weights, preferred_element_type=jnp.flo...]
    reduce_scatter x1 -> x0, waiting for transfers between devices: 102 us -> none  [on_device(): lax.psum_scatter(histogram_of(codes, weights), 'feat', scatter_dimension=...]
    pallas_call x0 -> x2, Pallas kernels: none -> 68.1 us  [the longest x1 66.8 us: on_device(): pl.pallas_call(kernel, out_shape=outs, in_specs=[pl.BlockSpec(memory_spac...]
    all_gather x1 -> x0, waiting for transfers between devices: 39.6 us -> none  [over_pieces(): return lax.all_gather(array, axis).sum(0)]
    all_to_all x1 -> x0, blocking collectives: 18.8 us -> none  [from_everyone(): lax.all_to_all(jnp.broadcast_to(array[None], (count, *array.shape)), axis...]
    eq x16 -> x0, local copies, waits for them, and re-layouts: 15.5 us -> none  [one_block(): onehot = (column_block[:, :, None] == bin_index).astype(jnp.bfloat16)]
    unnamed x9 -> x0, local copies, waits for them, and re-layouts: 5.46 us -> none
  transfers between devices with their start and end apart: 2 -> 0, of which waited for: 2 -> 0; matrix products, arithmetic and copies ran while one was open for 0% -> 0% of each run, Pallas kernels for 0% -> 0%
where the time goes in v2:
time: 68.9 us; the launch traced here: 68.8 us
  Pallas kernels  68.1 us (99%)
    pallas_call x1, Pallas kernels, on_device(): pl.pallas_call(kernel, out_shape=outs, in_specs=[pl.BlockSpec(memory_spac...  66.8 us

profile of v2, /device:TPU:1, one launch (start us, length us, event | category | flops | bytes accessed | tf_op | source)
XLA Modules:
  0.0 68.8 jit_solution(2522582093181535160)
XLA Ops:
  0.6 66.8 %shard_map.59 = (f32[2,4,16]{2,1,0:T(4,128)}, f32[2,4]{1,0:T(2,128)}) custom-call(s32[2048,512]{1,0:T(8,128)} %codes_hbm.1, s32[2,2048]{1,0:T(2,128)} %node_hbm.1, s32[2,2048]{1,0:T(2,128)} %bag_hbm.1, s32[1,2048]{1,0:T(1,128)} %bitcast.1), custom_call_target="tpu_custom_call" | custom-call | tf_op jit(solution)/shard_map/pallas_call | solution.py:412
  67.5 1.3 %shard_map.60 = (f32[2,4,16]{2,1,0:T(4,128)}, f32[2,4]{1,0:T(2,128)}) custom-call(f32[2,4,16]{2,1,0:T(4,128)} %get-tuple-element.4.feature_in, f32[2,4]{1,0:T(2,128)} %get-tuple-element.5.best_in), custom_call_target="tpu_custom_call" | custom-call | tf_op jit(solution)/shard_map/pallas_call | solution.py:456

commit v3 on v2

--- a/solution.py
+++ b/solution.py
@@ -16,6 +16,8 @@
 STEPS = 8
 TILE = 256
 LOAD = 512
+HALVES = 2 * STEPS
+LAG_A, LAG_B, LAG_Z = 3, 6, 10
 SCALE = 4096.0
 HIGH = lax.Precision.HIGHEST
 
@@ -243,6 +245,9 @@
     arrived(weight_in, weight_came)
     keep_weights(1, weight_in[:8], weight_in[8:])
 
+    def parts_of(u):
+        return 2 * (u // 4) + lax.rem(u, 2), lax.rem(u // 2, 2)
+
     def near(t, axis, way):
         on_y = lax.rem(t + axis, 2)
         on_x = 1 - on_y
@@ -255,54 +260,62 @@
         here = on_y * y + (1 - on_y) * x
         return lax.rem(here + shift + SIDE, SIDE)
 
-    def block(t, a, b=0):
+    def block(t, a, b):
         return t * 16 + a * 4 + b
 
-    def send(t, stage, src, dst, device):
+    def send(u, stage, src, dst, device):
         pltpu.make_async_remote_copy(
-            src, dst, block_sent, block_came.at[t, stage],
+            src, dst, block_sent, block_came.at[u, stage],
             device_id=device, device_id_type=MESH,
         ).start()
 
-    def two(first):
-        return pl.ds(first, 2)
-
-    def a1(t):
+    def a1(u):
+        t, h = parts_of(u)
         right, left = near(t, 0, 1), near(t, 0, -1)
-        far, r, l = (block(t, spot(t, 0, shift)) for shift in (2, 1, -1))
-        send(t, 0, hist.at[two(far)], a1_in.at[t, 0], right)
-        send(t, 0, hist.at[two(far + 2)], a1_in.at[t, 1], left)
-        send(t, 1, hist.at[two(r + 2)], a2_in.at[t, 0, two(2)], right)
-        send(t, 1, hist.at[two(l)], a2_in.at[t, 1, two(0)], left)
-
-    def a2(t):
-        arrived(a1_in.at[t], block_came.at[t, 0])
-        r, l = block(t, spot(t, 0, 1)), block(t, spot(t, 0, -1))
-        hist[two(r)] = hist[two(r)] + a1_in[t, 0]
-        hist[two(l + 2)] = hist[two(l + 2)] + a1_in[t, 1]
-        send(t, 1, hist.at[two(r)], a2_in.at[t, 0, two(0)], near(t, 0, 1))
-        send(t, 1, hist.at[two(l + 2)], a2_in.at[t, 1, two(2)], near(t, 0, -1))
-
-    def b1(t):
-        arrived(a2_in.at[t], block_came.at[t, 1])
-        first = block(t, spot(t, 0, 0))
-        mine = pl.ds(first, 4)
-        hist[mine] = hist[mine] + (a2_in[t, 0] + a2_in[t, 1])
-        for i, shift in enumerate((2, 1, -1)):
-            send(t, 2, hist.at[first + spot(t, 1, shift)], b_in.at[t, i], near(t, 1, shift))
-
-    def plane_sum(t):
-        arrived(b_in.at[t], block_came.at[t, 2])
+        far, r, l = (block(t, spot(t, 0, shift), 2 * h) for shift in (2, 1, -1))
+        send(u, 0, hist.at[far], a1_in.at[u, 0], right)
+        send(u, 0, hist.at[far + 1], a1_in.at[u, 1], left)
+        send(u, 1, hist.at[r + 1], a2_in.at[u, 0, 1], right)
+        send(u, 1, hist.at[l], a2_in.at[u, 1, 0], left)
+
+    def a2(u):
+        t, h = parts_of(u)
+        arrived(a1_in.at[u], block_came.at[u, 0])
+        r, l = (block(t, spot(t, 0, shift), 2 * h) for shift in (1, -1))
+        hist[r] = hist[r] + a1_in[u, 0]
+        hist[l + 1] = hist[l + 1] + a1_in[u, 1]
+        send(u, 1, hist.at[r], a2_in.at[u, 0, 0], near(t, 0, 1))
+        send(u, 1, hist.at[l + 1], a2_in.at[u, 1, 1], near(t, 0, -1))
+
+    def b1(u):
+        t, h = parts_of(u)
+        arrived(a2_in.at[u], block_came.at[u, 1])
+        first = block(t, spot(t, 0, 0), 2 * h)
+        mine = pl.ds(first, 2)
+        hist[mine] = hist[mine] + (a2_in[u, 0] + a2_in[u, 1])
+        for e in range(2):
+            away = lax.rem(2 * h + e - spot(t, 1, 0) + SIDE, SIDE)
+
+            @pl.when(away > 0)
+            def _():
+                send(u, 2, hist.at[first + e], b_in.at[u, away - 1], near(t, 1, away))
+
+    def plane_sum(u, t):
+        arrived(b_in.at[u], block_came.at[u, 2])
         mine = block(t, spot(t, 0, 0), spot(t, 1, 0))
-        return mine, (hist[mine] + b_in[t, 0]) + (b_in[t, 1] + b_in[t, 2])
-
-    def to_owner(t):
-        mine, value = plane_sum(t)
-        hist[mine] = value
-        pltpu.make_async_remote_copy(
-            hist.at[mine], z_in.at[t], block_sent, z_came,
-            device_id=(lax.rem(z + 1 + t, Z), q), device_id_type=MESH,
-        ).start()
+        return mine, (hist[mine] + b_in[u, 0]) + (b_in[u, 1] + b_in[u, 2])
+
+    def to_owner(u):
+        t, h = parts_of(u)
+
+        @pl.when((spot(t, 1, 0) // 2 == h) & (t < STEPS - 1))
+        def _():
+            mine, value = plane_sum(u, t)
+            hist[mine] = value
+            pltpu.make_async_remote_copy(
+                hist.at[mine], z_in.at[t], block_sent, z_came,
+                device_id=(lax.rem(z + 1 + t, Z), q), device_id_type=MESH,
+            ).start()
 
     count = iota((16, TILE), 0).astype(F32)
     numbers = [(count + 16.0 * m).astype(BF) for m in range(2)]
@@ -311,57 +324,55 @@
     passes = 2 * rows // TILE
     span = 1024 // TILE
 
-    def histogram(t, begin, end):
-        def some(i):
-            for u in range(2):
-                group = t * 8 + i * 2 + u
-                counts = None
-                for first in range(0, passes, span):
-                    total = None
-                    for k in range(first, first + span):
-                        source, lane = divmod(k * TILE, rows)
-                        cols = slice(lane, lane + TILE)
-                        upper, lower = sides(
-                            hi_ref, lo_ref, weight_ref[source, :, cols],
-                            scale_ref[source, :, cols], source, group * 4, lane, numbers, quads,
-                        )
-                        part = lax.dot_general(
-                            upper, lower, (((1,), (1,)), ((), ())), preferred_element_type=F32
-                        )
-                        total = part if total is None else total + part
-                    more = classes(total)
-                    counts = more if counts is None else [a + b for a, b in zip(counts, more)]
-                for e in range(2):
-                    hist[group * 2 + e, 0:32] = counts[2 * e]
-                    hist[group * 2 + e, 32:64] = counts[2 * e + 1]
-
-        loop(begin, end, some)
-
-    def step(t):
-        piece = pl.ds(pl.multiple_of(t * 32, 32), 32)
-        arrived(codes_in.at[piece], code_came.at[t])
-        hi, lo = split(codes_in[piece])
-        hi_ref[1, piece] = hi
-        lo_ref[1, piece] = lo
-        histogram(t, 0, 2)
-        pl.when(t >= 2)(lambda: a2(t - 2))
-        pl.when(t >= 5)(lambda: to_owner(t - 5))
-        histogram(t, 2, 4)
-        a1(t)
-        pl.when(t >= 3)(lambda: b1(t - 3))
-
-    loop(0, STEPS, step)
+    def count_group(group):
+        counts = None
+        for first in range(0, passes, span):
+            total = None
+            for k in range(first, first + span):
+                source, lane = divmod(k * TILE, rows)
+                cols = slice(lane, lane + TILE)
+                upper, lower = sides(
+                    hi_ref, lo_ref, weight_ref[source, :, cols],
+                    scale_ref[source, :, cols], source, group * 4, lane, numbers, quads,
+                )
+                part = lax.dot_general(
+                    upper, lower, (((1,), (1,)), ((), ())), preferred_element_type=F32
+                )
+                total = part if total is None else total + part
+            more = classes(total)
+            counts = more if counts is None else [a + b for a, b in zip(counts, more)]
+        for e in range(2):
+            hist[group * 2 + e, 0:32] = counts[2 * e]
+            hist[group * 2 + e, 32:64] = counts[2 * e + 1]
+
+    def half_step(u):
+        t, h = parts_of(u)
+
+        @pl.when(h == 0)
+        def _():
+            piece = pl.ds(pl.multiple_of(t * 32, 32), 32)
+            arrived(codes_in.at[piece], code_came.at[t])
+            hi, lo = split(codes_in[piece])
+            hi_ref[1, piece] = hi
+            lo_ref[1, piece] = lo
+
+        for a in range(SIDE):
+            count_group(t * 8 + 2 * a + h)
+        pl.when(u >= LAG_B)(lambda: b1(u - LAG_B))
+        pl.when(u >= LAG_A)(lambda: a2(u - LAG_A))
+        a1(u)
+        pl.when(u >= LAG_Z)(lambda: to_owner(u - LAG_Z))
+
+    loop(0, HALVES, half_step)
+
+    def finish(u):
+        pl.when(u < HALVES + LAG_B)(lambda: b1(u - LAG_B))
+        pl.when(u < HALVES + LAG_A)(lambda: a2(u - LAG_A))
+        pl.when(u < HALVES + LAG_Z)(lambda: to_owner(u - LAG_Z))
+
+    loop(HALVES, HALVES + LAG_Z, finish)
     last = STEPS - 1
-    a2(last - 1)
-    to_owner(last - 4)
-    b1(last - 2)
-    a2(last)
-    to_owner(last - 3)
-    b1(last - 1)
-    to_owner(last - 2)
-    b1(last)
-    to_owner(last - 1)
-    _, summed = plane_sum(last)
+    _, summed = plane_sum(HALVES - 3 + 2 * (spot(last, 1, 0) // 2), last)
     arrived(z_in, z_came)
     summed = summed + jnp.sum(z_in[...], axis=0)
     own_gain[...] = gains(summed, z)
@@ -428,9 +439,9 @@
             pltpu.VMEM((16, rows), F32),
             pltpu.VMEM((16, rows), F32),
             pltpu.VMEM((STEPS * 16, 64, 128), F32),
-            pltpu.VMEM((STEPS, 2, 2, 64, 128), F32),
-            pltpu.VMEM((STEPS, 2, 4, 64, 128), F32),
-            pltpu.VMEM((STEPS, 3, 64, 128), F32),
+            pltpu.VMEM((HALVES, 2, 64, 128), F32),
+            pltpu.VMEM((HALVES, 2, 2, 64, 128), F32),
+            pltpu.VMEM((HALVES, 3, 64, 128), F32),
             pltpu.VMEM((STEPS - 1, 64, 128), F32),
             pltpu.VMEM((8, 128), F32),
             pltpu.VMEM((Z - 1, 8, 128), F32),
@@ -444,7 +455,7 @@
             dma(()),
             dma((STEPS,)),
             dma(()),
-            dma((STEPS, 3)),
+            dma((HALVES, 3)),
             dma(()),
             dma(()),
             dma(()),

time: 68.9 us -> 64.3 us (0.933)
  Pallas kernels: 68.1 us -> 63.6 us
    pallas_call x1, Pallas kernels: 66.8 us -> 62.3 us  [on_device(): pl.pallas_call(kernel, out_shape=outs, in_specs=[pl.BlockSpec(memory_spac...]
where the time goes in v3:
time: 64.3 us; the launch traced here: 64.2 us
  Pallas kernels  63.6 us (99%)
    pallas_call x1, Pallas kernels, on_device(): pl.pallas_call(kernel, out_shape=outs, in_specs=[pl.BlockSpec(memory_spac...  62.3 us

profile of v3, /device:TPU:1, one launch (start us, length us, event | category | flops | bytes accessed | tf_op | source)
XLA Modules:
  0.0 64.2 jit_solution(1502956509876215027)
XLA Ops:
  0.6 62.3 %shard_map.59 = (f32[2,4,16]{2,1,0:T(4,128)}, f32[2,4]{1,0:T(2,128)}) custom-call(s32[2048,512]{1,0:T(8,128)} %codes_hbm.1, s32[2,2048]{1,0:T(2,128)} %node_hbm.1, s32[2,2048]{1,0:T(2,128)} %bag_hbm.1, s32[1,2048]{1,0:T(1,128)} %bitcast.1), custom_call_target="tpu_custom_call" | custom-call | tf_op jit(solution)/shard_map/pallas_call | solution.py:423
  62.9 1.3 %shard_map.60 = (f32[2,4,16]{2,1,0:T(4,128)}, f32[2,4]{1,0:T(2,128)}) custom-call(f32[2,4,16]{2,1,0:T(4,128)} %get-tuple-element.4.feature_in, f32[2,4]{1,0:T(2,128)} %get-tuple-element.5.best_in), custom_call_target="tpu_custom_call" | custom-call | tf_op jit(solution)/shard_map/pallas_call | solution.py:467

commit v4 on v3

--- a/solution.py
+++ b/solution.py
@@ -15,7 +15,7 @@
 SIDE = 4
 STEPS = 8
 TILE = 256
-LOAD = 512
+LOAD = 1024
 HALVES = 2 * STEPS
 LAG_A, LAG_B, LAG_Z = 3, 6, 10
 SCALE = 4096.0
@@ -246,7 +246,9 @@
     keep_weights(1, weight_in[:8], weight_in[8:])
 
     def parts_of(u):
-        return 2 * (u // 4) + lax.rem(u, 2), lax.rem(u // 2, 2)
+        ends = u >= HALVES - 4
+        t = jnp.where(ends, u // 2, 2 * (u // 4) + lax.rem(u, 2))
+        return t, jnp.where(ends, lax.rem(u, 2), lax.rem(u // 2, 2))
 
     def near(t, axis, way):
         on_y = lax.rem(t + axis, 2)
@@ -366,13 +368,13 @@
     loop(0, HALVES, half_step)
 
     def finish(u):
+        pl.when(u < HALVES + LAG_A)(lambda: a2(u - LAG_A))
         pl.when(u < HALVES + LAG_B)(lambda: b1(u - LAG_B))
-        pl.when(u < HALVES + LAG_A)(lambda: a2(u - LAG_A))
         pl.when(u < HALVES + LAG_Z)(lambda: to_owner(u - LAG_Z))
 
     loop(HALVES, HALVES + LAG_Z, finish)
     last = STEPS - 1
-    _, summed = plane_sum(HALVES - 3 + 2 * (spot(last, 1, 0) // 2), last)
+    _, summed = plane_sum(HALVES - 2 + spot(last, 1, 0) // 2, last)
     arrived(z_in, z_came)
     summed = summed + jnp.sum(z_in[...], axis=0)
     own_gain[...] = gains(summed, z)
@@ -393,7 +395,7 @@
     arrived(gain_in, gain_came)
     together = own_gain[...] + jnp.sum(gain_in[...], axis=0)
     own_best[...] = jnp.broadcast_to(jnp.max(together, axis=1, keepdims=True), (8, 128))
-    loop(1, Q, send_best)
+    loop(0, Q - 1, lambda i: send_best(lax.rem(i + 18, Q - 1) + 1))
     for tree in range(2):
         feature_ref[tree] = together[4 * tree : 4 * tree + 4, :16]
 

time: 64.3 us -> 63.4 us (0.986)
  Pallas kernels: 63.6 us -> 62.6 us
    pallas_call x1, Pallas kernels: 62.3 us -> 61.3 us  [on_device(): pl.pallas_call(kernel, out_shape=outs, in_specs=[pl.BlockSpec(memory_spac...]
where the time goes in v4:
time: 63.4 us; the launch traced here: 63.2 us
  Pallas kernels  62.6 us (99%)
  between operations  0.64 us (1%)
    pallas_call x1, Pallas kernels, on_device(): pl.pallas_call(kernel, out_shape=outs, in_specs=[pl.BlockSpec(memory_spac...  61.3 us
    pallas_call x1, Pallas kernels, on_device(): pl.pallas_call(hand_over, out_shape=outs, in_specs=[whole] * 2, out_specs...  1.27 us

profile of v4, /device:TPU:1, one launch (start us, length us, event | category | flops | bytes accessed | tf_op | source)
XLA Modules:
  0.0 63.2 jit_solution(4735808655606750743)
XLA Ops:
  0.6 61.3 %shard_map.59 = (f32[2,4,16]{2,1,0:T(4,128)}, f32[2,4]{1,0:T(2,128)}) custom-call(s32[2048,512]{1,0:T(8,128)} %codes_hbm.1, s32[2,2048]{1,0:T(2,128)} %node_hbm.1, s32[2,2048]{1,0:T(2,128)} %bag_hbm.1, s32[1,2048]{1,0:T(1,128)} %bitcast.1), custom_call_target="tpu_custom_call" | custom-call | tf_op jit(solution)/shard_map/pallas_call | solution.py:425
  62.0 1.3 %shard_map.60 = (f32[2,4,16]{2,1,0:T(4,128)}, f32[2,4]{1,0:T(2,128)}) custom-call(f32[2,4,16]{2,1,0:T(4,128)} %get-tuple-element.4.feature_in, f32[2,4]{1,0:T(2,128)} %get-tuple-element.5.best_in), custom_call_target="tpu_custom_call" | custom-call | tf_op jit(solution)/shard_map/pallas_call | solution.py:469

commit v5 on v4

--- a/solution.py
+++ b/solution.py
@@ -360,9 +360,9 @@
 
         for a in range(SIDE):
             count_group(t * 8 + 2 * a + h)
-        pl.when(u >= LAG_B)(lambda: b1(u - LAG_B))
         pl.when(u >= LAG_A)(lambda: a2(u - LAG_A))
         a1(u)
+        pl.when(u >= LAG_B)(lambda: b1(u - LAG_B))
         pl.when(u >= LAG_Z)(lambda: to_owner(u - LAG_Z))
 
     loop(0, HALVES, half_step)

time: 63.4 us -> 63.2 us (level)
  no operation moved by 1% of the time
where the time goes in v5:
time: 63.2 us; the launch traced here: 63.1 us
  Pallas kernels  62.4 us (99%)
  between operations  0.64 us (1%)
    pallas_call x1, Pallas kernels, on_device(): pl.pallas_call(kernel, out_shape=outs, in_specs=[pl.BlockSpec(memory_spac...  61.1 us
    pallas_call x1, Pallas kernels, on_device(): pl.pallas_call(hand_over, out_shape=outs, in_specs=[whole] * 2, out_specs...  1.27 us

profile of v5, /device:TPU:1, one launch (start us, length us, event | category | flops | bytes accessed | tf_op | source)
XLA Modules:
  0.0 63.1 jit_solution(3621752786868864364)
XLA Ops:
  0.6 61.1 %shard_map.59 = (f32[2,4,16]{2,1,0:T(4,128)}, f32[2,4]{1,0:T(2,128)}) custom-call(s32[2048,512]{1,0:T(8,128)} %codes_hbm.1, s32[2,2048]{1,0:T(2,128)} %node_hbm.1, s32[2,2048]{1,0:T(2,128)} %bag_hbm.1, s32[1,2048]{1,0:T(1,128)} %bitcast.1), custom_call_target="tpu_custom_call" | custom-call | tf_op jit(solution)/shard_map/pallas_call | solution.py:425
  61.8 1.3 %shard_map.60 = (f32[2,4,16]{2,1,0:T(4,128)}, f32[2,4]{1,0:T(2,128)}) custom-call(f32[2,4,16]{2,1,0:T(4,128)} %get-tuple-element.4.feature_in, f32[2,4]{1,0:T(2,128)} %get-tuple-element.5.best_in), custom_call_target="tpu_custom_call" | custom-call | tf_op jit(solution)/shard_map/pallas_call | solution.py:469
